TPU v7x, 32 devices: a whole 2x2x4 slice. The times are simulated.
32 devices in a mesh: track: 16 (over z, y, x), cam: 2 (over core).
Axes of the slice: x: 2, y: 2, z: 4, core: 2. Of those that a mesh axis runs over, the one named last changes fastest.
Arguments:
- omega: bfloat16 [32, 9, 4096], P(None, None, ('track', 'cam')), may hold values from -6 to 6
- u_blocks: float32 [9, 9, 4096], P(None, None, ('track', 'cam')), may hold values from -5.4 to 36, as said below
- w_blocks: bfloat16 [9, 3, 16384], P(None, None, ('track', 'cam')), may hold values from -1.796875 to 1.796875
- v_inverse: float32 [3, 3, 4096], P(None, None, ('track', 'cam')), may hold values from -0.6 to 1.5, as said below
- obs_camera: int32 [16384], P(('track', 'cam')), may hold values from 0 to 4095, as said below
- obs_track: int32 [16384], P(('track', 'cam')), may hold values from 0 to 31, as said below
- obs_mask: int32 [16384], P(('track', 'cam')), may hold values from 0 to 1, as said below
Outputs:
- sketch: float32 [32, 9, 4096], P(None, None, ('track', 'cam'))
- basis: float32 [32, 9, 4096], P(None, None, ('track', 'cam'))
- factor: float32 [32, 32], replicated
Inputs may be any that keep to these rules, and one draw needn't show every extreme that they name: `obs_camera`: cameras c * 128 to (c + 1) * 128 - 1 belong to device c (track slower). Among one device's 512 observations, padding included, at most 32 name cameras of any one device, and exactly 32 name those of some device. `obs_track`: in each aligned block of 128 observations, slots 0 to 31 each hold one track of 2 to 4 consecutive observations from the block's start, in rising order; the padding after them carries slot 31. `obs_mask`: 1 on the observations of tracks, 0 on the padding at the end of each block. `u_blocks`: each block is symmetric. `v_inverse`: each block is symmetric positive definite.
All inputs are finite; a program needn't handle non-finite values.
Results may differ from a plain program's by a relative error of at most 0.00095.
Values may be sent and summed in bfloat16 or wider, within the bound.
A program may use at most 64 MiB of HBM per device.

v0:
```python
import jax
import jax.numpy as jnp
from jax import lax
from jax.sharding import PartitionSpec as P

BLK_OBS = 128
TRK_BLK = 32


HIGH = lax.Precision.HIGHEST


def eliminate(gathered, w_blocks, v_inverse, obs_track, obs_mask):
    weights = w_blocks.astype(jnp.float32)
    live_mask = obs_mask.astype(jnp.float32)
    values = gathered.astype(jnp.float32)
    columns = values.shape[1]
    obs_count = values.shape[2]
    blocks = obs_count // BLK_OBS
    projected = (
        jnp.stack(
            [
                sum(
                    (
                        weights[comp_row, comp_col][None, :] * values[comp_row]
                        for comp_row in range(9)
                    )
                )
                for comp_col in range(3)
            ]
        )
        * live_mask
    )
    member = (
        obs_track.reshape(blocks, BLK_OBS)[:, :, None] == jnp.arange(TRK_BLK, dtype=jnp.int32)
    ).astype(jnp.float32)
    summed = jnp.einsum(
        "icbo,bot->icbt", projected.reshape(3, columns, blocks, BLK_OBS), member, precision=HIGH
    ).reshape(3, columns, blocks * TRK_BLK)
    solved = jnp.stack(
        [
            sum(
                (v_inverse[comp_row, comp_col][None, :] * summed[comp_col] for comp_col in range(3))
            )
            for comp_row in range(3)
        ]
    )
    spread = jnp.einsum(
        "icbt,bot->icbo", solved.reshape(3, columns, blocks, TRK_BLK), member, precision=HIGH
    ).reshape(3, columns, obs_count)
    returned = (
        jnp.stack(
            [
                sum(
                    (
                        weights[comp_row, comp_col][None, :] * spread[comp_col]
                        for comp_col in range(3)
                    )
                )
                for comp_row in range(9)
            ]
        )
        * live_mask
    )
    return returned.astype(jnp.bfloat16)


def on_device(omega, u_blocks, w_blocks, v_inverse, obs_camera, obs_track, obs_mask):
    track_count = lax.axis_size("track")
    cam_count = lax.axis_size("cam")
    devices = track_count * cam_count
    columns, params, cam_width = omega.shape
    obs_count = obs_camera.shape[0]
    capacity = max(2, 2 * obs_count // devices)
    buffer_slots = devices * capacity
    owner_index = obs_camera // cam_width
    ordering = jnp.argsort(owner_index, stable=True)
    ranked = owner_index[ordering]
    first_index = jnp.searchsorted(ranked, ranked, side="left")
    placed = ranked * capacity + jnp.arange(obs_count, dtype=jnp.int32) - first_index
    slot_index = jnp.zeros((obs_count,), jnp.int32).at[ordering].set(placed)
    request = (
        jnp.full((buffer_slots,), -1, jnp.int32)
        .at[slot_index]
        .set(obs_camera)
        .reshape(track_count, cam_count, capacity)
    )
    camera_ids = lax.all_to_all(
        lax.all_to_all(request, "track", split_axis=0, concat_axis=0, tiled=True),
        "cam",
        split_axis=1,
        concat_axis=1,
        tiled=True,
    )
    table_start = (lax.axis_index("track") * cam_count + lax.axis_index("cam")) * cam_width
    table_width = omega.shape[2]
    is_live = camera_ids >= 0
    local_ids = jnp.where(is_live, camera_ids - table_start, 0).reshape(-1)
    gathered_rows = jnp.take(omega, local_ids, axis=2)
    outgoing = (
        gathered_rows.reshape(columns, params, track_count, cam_count, capacity)
        .transpose(2, 3, 1, 4, 0)
        .reshape(track_count, cam_count, params, capacity * columns)
    )
    returned = lax.all_to_all(
        lax.all_to_all(outgoing, "track", split_axis=0, concat_axis=0, tiled=True),
        "cam",
        split_axis=1,
        concat_axis=1,
        tiled=True,
    )
    received = (
        returned.reshape(track_count, cam_count, params, capacity, columns)
        .transpose(2, 4, 0, 1, 3)
        .reshape(params, columns, buffer_slots)
    )
    needed = jnp.take(received, slot_index, axis=2)
    contribution = eliminate(needed, w_blocks, v_inverse, obs_track, obs_mask)
    buffer = (
        jnp.zeros((params, columns, buffer_slots), jnp.bfloat16)
        .at[:, :, slot_index]
        .set(contribution)
    )
    packed = (
        buffer.reshape(params, columns, track_count, cam_count, capacity)
        .transpose(2, 3, 0, 4, 1)
        .reshape(track_count, cam_count, params, capacity * columns)
    )
    arrived = lax.all_to_all(
        lax.all_to_all(packed, "track", split_axis=0, concat_axis=0, tiled=True),
        "cam",
        split_axis=1,
        concat_axis=1,
        tiled=True,
    )
    terms = (
        arrived.reshape(track_count, cam_count, params, capacity, columns)
        .transpose(4, 2, 0, 1, 3)
        .reshape(columns, params, buffer_slots)
        .astype(jnp.float32)
    )
    target = jnp.where(is_live, camera_ids - table_start, table_width).reshape(-1)
    incoming = (
        jnp.zeros((columns, params, table_width + 1), jnp.float32)
        .at[:, :, target]
        .add(terms)[:, :, :table_width]
    )
    own_term = jnp.einsum("mnk,jnk->jmk", u_blocks, omega.astype(jnp.float32), precision=HIGH)
    sketch = own_term - incoming
    flat_rows = sketch.reshape(columns, params * cam_width)
    gram_local = jnp.dot(flat_rows, flat_rows.T, precision=HIGH, preferred_element_type=jnp.float32)
    row_total = params * cam_width * devices
    lower_factor = jnp.linalg.cholesky(lax.psum(gram_local, ("track", "cam")) / row_total)
    basis_rows = jax.scipy.linalg.solve_triangular(lower_factor, flat_rows, lower=True).reshape(
        sketch.shape
    )
    return (sketch, basis_rows, lower_factor.T)


def solution(mesh):
    in_specs = (
        P(None, None, ("track", "cam")),
        P(None, None, ("track", "cam")),
        P(None, None, ("track", "cam")),
        P(None, None, ("track", "cam")),
        P(("track", "cam")),
        P(("track", "cam")),
        P(("track", "cam")),
    )
    out_specs = (P(None, None, ("track", "cam")), P(None, None, ("track", "cam")), P())
    return jax.shard_map(
        on_device, mesh=mesh, in_specs=in_specs, out_specs=out_specs, check_vma=False
    )
```

profile of v0, /device:TPU:0, one launch (start us, length us, event | category | flops | bytes accessed | tf_op | source)
XLA Modules:
  0.0 364.1 jit_solution(12495128076649908816)
XLA Ops:
  1.3 3.8 %sort.17 = (s32[512]{0:T(512)}, s32[512]{0:T(512)S(1)}) sort(s32[512]{0:T(512)S(1)} %add_select_fusion, s32[512]{0:T(512)S(1)} %iota.38), dimensions={0}, to_apply=%region_0.1 | sort | flops 4608 | bytes 8192 | tf_op jit(solution)/shard_map/jit(argsort)/sort | solution.py:77
  5.1 3.5 gather_fusion.1
  8.6 35.9 %while.25 = (s32[]{:T(128)}, u32[512]{0:T(512)S(1)}, u32[512]{0:T(512)S(1)}, s32[512]{0:T(512)S(1)}, s32[]{:T(128)}, /*index=5*/s32[]{:T(128)}, s32[]{}) while((s32[]{:T(128)}, u32[512]{0:T(512)S(1)}, u32[512]{0:T(512)S(1)}, s32[512]{0:T(512)S(1)}, s32[]{:T(128)}, /*index=5*/s32[]{:T(128)}, s32[]{}) %tuple.87), condition=%wide.region_2.3_spmd.clone, body=%wide.region_1.2_spmd.clone.sunk | while | flops 10244 | bytes 40037 | solution.py:79
  8.7 3.5 gather_fusion
  12.3 3.5 gather_fusion
  15.9 3.5 gather_fusion
  19.4 3.5 gather_fusion
  23.0 3.5 gather_fusion
  26.6 3.5 gather_fusion
  30.2 3.5 gather_fusion
  33.8 3.5 gather_fusion
  37.4 3.5 gather_fusion
  41.0 3.5 gather_fusion
  44.5 2.4 scatter_custom_fusion
  47.0 2.6 scatter_custom_fusion.1
  50.3 8.3 %all-to-all-start = ((s32[16,2,32]{2,1,0:T(2,128)}), s32[16,2,32]{2,1,0:T(2,128)S(1)}, u32[]{:S(2)}, u32[]{:S(2)}) async-start(s32[16,2,32]{2,1,0:T(2,128)} %reshape.1434), calls=%async_computation | async-start | bytes 32768 | tf_op jit(solution)/shard_map/all_to_all | solution.py:89
  59.1 6.9 %all-to-all-done = s32[16,2,32]{2,1,0:T(2,128)S(1)} async-done(((s32[16,2,32]{2,1,0:T(2,128)}), s32[16,2,32]{2,1,0:T(2,128)S(1)}, u32[]{:S(2)}, u32[]{:S(2)}) %all-to-all-start) | async-done | bytes 4128 | tf_op jit(solution)/shard_map/all_to_all | solution.py:89
  66.1 3.7 %all_to_all.30 = s32[2,1,512]{2,1,0:T(1,128)S(1)} all-to-all(s32[2,1,512]{2,1,0:T(1,128)S(1)} %reshape.1574), channel_id=1, replica_groups=mesh['track'=16,'cam'=2] {'cam'}, dimensions={0} | all-to-all | bytes 8192 | tf_op jit(solution)/shard_map/all_to_all | solution.py:88
  71.2 8.3 %gather_fusion.2 = bf16[1024,32,9]{1,2,0:T(8,128)(2,1)} fusion(bf16[32,9,128]{0,1,2:T(8,128)(2,1)S(1)} %copy.264, s32[1024]{0:T(1024)S(1)} %broadcast_clamp_fusion), kind=kCustom, calls=%fused_computation.2 | custom fusion | bytes 1183744 | tf_op jit(solution)/shard_map/jit(_take)/gather | solution.py:99
  79.5 2.8 fusion
  82.3 2.5 reshape.1437
  84.7 1.4 copy.271
  86.2 3.6 all-to-all-start.2
  98.8 7.5 %all-to-all-done.2 = bf16[16,2,9,1024]{3,1,2,0:T(2,128)(2,1)S(1)} async-done(((bf16[16,2,9,1024]{3,1,2,0:T(2,128)(2,1)}), bf16[16,2,9,1024]{3,1,2,0:T(2,128)(2,1)S(1)}, u32[]{:S(2)}, u32[]{:S(2)}) %all-to-all-start.2) | async-done | bytes 589856 | tf_op jit(solution)/shard_map/all_to_all | solution.py:106
  106.5 4.2 %all_to_all.31 = bf16[16,2,9,1024]{3,0,2,1:T(8,128)(2,1)S(1)} all-to-all(bf16[16,2,9,1024]{3,0,2,1:T(8,128)(2,1)S(1)} %copy.272), channel_id=1, replica_groups=mesh['track'=16,'cam'=2] {'cam'}, dimensions={1} | all-to-all | bytes 1179648 | tf_op jit(solution)/shard_map/all_to_all | solution.py:105
  110.7 1.8 reshape.1438
  112.5 4.9 %copy.328 = bf16[9,32,16,2,32]{1,0,4,3,2:T(8,128)(2,1)} copy(bf16[9,32,16,2,32]{1,4,2,0,3:T(8,128)(2,1)S(1)} %bitcast.143) | data formatting | bytes 1179648 | tf_op jit(solution)/shard_map/reshape | solution.py:115
  117.6 3.4 gather_fusion.3
  121.1 1.2 copy.275
  124.4 2.0 copy.310
  126.4 2.5 broadcast_in_dim.74
  128.9 47.4 %scatter_fusion = bf16[9,32,1024]{1,0,2:T(8,128)(2,1)} fusion(bf16[9,32,1024]{1,0,2:T(8,128)(2,1)} %broadcast_in_dim.74, s32[512]{0:T(512)S(1)} %copy-done.25, bf16[512,9,32]{2,1,0:T(8,128)(2,1)S(1)} %copy.310), kind=kCustom, calls=%fused_computation.6 | custom fusion | bytes 886784 | tf_op jit(solution)/shard_map/scatter | solution.py:122
  176.3 2.8 copy.379
  179.1 2.5 reshape.1441
  181.6 1.4 copy.312
  183.0 4.4 %all-to-all-start.4 = ((bf16[16,2,9,1024]{3,1,2,0:T(2,128)(2,1)}), bf16[16,2,9,1024]{3,1,2,0:T(2,128)(2,1)S(1)}, u32[]{:S(2)}, u32[]{:S(2)}) async-start(bf16[16,2,9,1024]{3,1,2,0:T(2,128)(2,1)} %copy.312), calls=%async_computation.4 | async-start | bytes 1179648 | tf_op jit(solution)/shard_map/all_to_all | solution.py:130
  187.5 1.4 copy.265
  189.0 15.0 %all-to-all-done.4 = bf16[16,2,9,1024]{3,1,2,0:T(2,128)(2,1)S(1)} async-done(((bf16[16,2,9,1024]{3,1,2,0:T(2,128)(2,1)}), bf16[16,2,9,1024]{3,1,2,0:T(2,128)(2,1)S(1)}, u32[]{:S(2)}, u32[]{:S(2)}) %all-to-all-start.4) | async-done | bytes 589856 | tf_op jit(solution)/shard_map/all_to_all | solution.py:130
  204.1 4.2 %all_to_all.32 = bf16[16,2,9,1024]{3,0,2,1:T(8,128)(2,1)S(1)} all-to-all(bf16[16,2,9,1024]{3,0,2,1:T(8,128)(2,1)S(1)} %copy.313), channel_id=1, replica_groups=mesh['track'=16,'cam'=2] {'cam'}, dimensions={1} | all-to-all | bytes 1179648 | tf_op jit(solution)/shard_map/all_to_all | solution.py:129
  208.4 2.8 reshape.1444
  211.2 7.7 %copy.314 = f32[32,9,16,2,32]{4,3,2,0,1:T(2,128)} copy(f32[32,9,16,2,32]{0,4,2,1,3:T(8,128)} %bitcast.141) | data formatting | bytes 2359296 | tf_op jit(solution)/shard_map/convert_element_type | solution.py:140
  218.9 6.9 %reshape.1502 = f32[32,9,1024]{2,0,1:T(8,128)S(1)} reshape(f32[32,9,16,2,32]{4,3,2,0,1:T(2,128)} %copy.314) | data formatting | bytes 2359296 | tf_op jit(solution)/shard_map/convert_element_type | solution.py:140
  225.8 6.1 %copy.315 = f32[1024,32,9]{1,2,0:T(8,128)} copy(f32[1024,32,9]{0,1,2:T(8,128)S(1)} %bitcast.174) | data formatting | bytes 2359296 | tf_op jit(solution)/shard_map/convert_element_type | solution.py:140
  232.0 81.1 %scatter_fusion.1 = f32[32,9,129]{0,1,2:T(8,128)S(1)} fusion(f32[32,9,129]{0,1,2:T(8,128)S(1)} %broadcast_in_dim.67, s32[1024]{0:T(1024)S(1)} %bitcast.234, f32[1024,32,9]{1,2,0:T(8,128)} %copy.315), kind=kCustom, calls=%fused_computation.7 | custom fusion | flops 294912 | bytes 3543040 | tf_op jit(solution)/shard_map/scatter-add | solution.py:146
  313.1 1.9 fusion.1
  316.1 39.5 %psum.7 = f32[32,32]{0,1:T(8,128)S(1)} all-reduce(f32[32,32]{0,1:T(8,128)S(1)} %convolution_bitcast_fusion.2), channel_id=1, replica_groups=mesh['track'=16,'cam'=2] {'track','cam'}, use_global_device_ids=true, to_apply=%region_7.8 | all-reduce | flops 1024 | bytes 8192 | tf_op jit(solution)/shard_map/psum | solution.py:153
  355.7 2.9 cholesky.16
  359.9 2.4 custom-call.7
  (209 shorter events, 19.2 us)
Async XLA Ops:
  8.6 50.0 %copy-start.2 = (bf16[32,9,128]{2,0,1:T(8,128)(2,1)S(1)}, bf16[32,9,128]{2,0,1:T(8,128)(2,1)}, u32[]{:S(2)}) copy-start(bf16[32,9,128]{2,0,1:T(8,128)(2,1)} %param.9) | copy-start | bytes 221188
  47.0 48.8 %copy-start.24 = (s32[512]{0:T(512)}, s32[512]{0:T(512)S(1)}, u32[]{:S(2)}) copy-start(s32[512]{0:T(512)S(1)} %compare_select_fusion.3) | copy-start | bytes 6148
  50.3 15.7 %all-to-all-start = ((s32[16,2,32]{2,1,0:T(2,128)}), s32[16,2,32]{2,1,0:T(2,128)S(1)}, u32[]{:S(2)}, u32[]{:S(2)}) async-start(s32[16,2,32]{2,1,0:T(2,128)} %reshape.1434), calls=%async_computation | async-start | bytes 32768 | tf_op jit(solution)/shard_map/all_to_all | solution.py:89
  82.2 7.5 %copy-start.39 = (f32[3,3,128]{2,1,0:T(4,128)S(1)}, f32[3,3,128]{2,1,0:T(4,128)}, u32[]{:S(2)}) copy-start(f32[3,3,128]{2,1,0:T(4,128)} %param.12) | copy-start | bytes 13828
  82.2 14.7 %copy-start.41 = (s32[512]{0:T(512)S(1)}, s32[512]{0:T(512)}, u32[]{:S(2)}) copy-start(s32[512]{0:T(512)} %param.15) | copy-start | bytes 6148
  82.2 15.3 %copy-start.1 = (bf16[9,3,512]{2,1,0:T(4,128)(2,1)S(1)}, bf16[9,3,512]{2,1,0:T(4,128)(2,1)}, u32[]{:S(2)}) copy-start(bf16[9,3,512]{2,1,0:T(4,128)(2,1)} %param.11) | copy-start | bytes 82948
  86.2 20.2 %all-to-all-start.2 = ((bf16[16,2,9,1024]{3,1,2,0:T(2,128)(2,1)}), bf16[16,2,9,1024]{3,1,2,0:T(2,128)(2,1)S(1)}, u32[]{:S(2)}, u32[]{:S(2)}) async-start(bf16[16,2,9,1024]{3,1,2,0:T(2,128)(2,1)} %copy.271), calls=%async_computation.2 | async-start | bytes 1179648 | tf_op jit(solution)/shard_map/all_to_all | solution.py:106
  112.5 5.1 %copy-start.26 = (s32[1024]{0:T(1024)S(1)}, s32[1024]{0:T(1024)}, u32[]{:S(2)}) copy-start(s32[1024]{0:T(1024)} %pad_clamp_fusion.1) | copy-start | bytes 12292
  117.4 4.9 %copy-start.40 = (pred[512]{0:T(512)(128)(4,1)S(1)}, pred[512]{0:T(512)(128)(4,1)}, u32[]{:S(2)}) copy-start(pred[512]{0:T(512)(128)(4,1)} %compare_and_fusion.1) | copy-start | bytes 1540
  117.4 5.0 %copy-start.5 = (f32[1,1,512]{2,1,0:T(1,128)S(1)}, f32[1,1,512]{2,1,0:T(1,128)}, u32[]{:S(2)}) copy-start(f32[1,1,512]{2,1,0:T(1,128)} %get-tuple-element.140) | copy-start | bytes 6148
  117.4 5.0 %copy-start.8 = (f32[1,1,512]{2,1,0:T(1,128)S(1)}, f32[1,1,512]{2,1,0:T(1,128)}, u32[]{:S(2)}) copy-start(f32[1,1,512]{2,1,0:T(1,128)} %get-tuple-element.139) | copy-start | bytes 6148
  117.4 5.0 %copy-start.10 = (f32[1,1,512]{2,1,0:T(1,128)S(1)}, f32[1,1,512]{2,1,0:T(1,128)}, u32[]{:S(2)}) copy-start(f32[1,1,512]{2,1,0:T(1,128)} %get-tuple-element.138) | copy-start | bytes 6148
  117.4 5.0 %copy-start.13 = (f32[1,1,512]{2,1,0:T(1,128)S(1)}, f32[1,1,512]{2,1,0:T(1,128)}, u32[]{:S(2)}) copy-start(f32[1,1,512]{2,1,0:T(1,128)} %get-tuple-element.137) | copy-start | bytes 6148
  117.4 5.0 %copy-start.15 = (f32[1,1,512]{2,1,0:T(1,128)S(1)}, f32[1,1,512]{2,1,0:T(1,128)}, u32[]{:S(2)}) copy-start(f32[1,1,512]{2,1,0:T(1,128)} %get-tuple-element.136) | copy-start | bytes 6148
  117.4 5.0 %copy-start.17 = (f32[1,1,512]{2,1,0:T(1,128)S(1)}, f32[1,1,512]{2,1,0:T(1,128)}, u32[]{:S(2)}) copy-start(f32[1,1,512]{2,1,0:T(1,128)} %get-tuple-element.135) | copy-start | bytes 6148
  117.4 5.0 %copy-start.19 = (f32[1,1,512]{2,1,0:T(1,128)S(1)}, f32[1,1,512]{2,1,0:T(1,128)}, u32[]{:S(2)}) copy-start(f32[1,1,512]{2,1,0:T(1,128)} %get-tuple-element.134) | copy-start | bytes 6148
  117.5 5.0 %copy-start.21 = (f32[1,1,512]{2,1,0:T(1,128)S(1)}, f32[1,1,512]{2,1,0:T(1,128)}, u32[]{:S(2)}) copy-start(f32[1,1,512]{2,1,0:T(1,128)} %get-tuple-element.133) | copy-start | bytes 6148
  117.5 5.0 %copy-start.4 = (f32[1,1,512]{2,1,0:T(1,128)S(1)}, f32[1,1,512]{2,1,0:T(1,128)}, u32[]{:S(2)}) copy-start(f32[1,1,512]{2,1,0:T(1,128)} %get-tuple-element.154) | copy-start | bytes 6148
  117.5 5.0 %copy-start.6 = (f32[1,1,512]{2,1,0:T(1,128)S(1)}, f32[1,1,512]{2,1,0:T(1,128)}, u32[]{:S(2)}) copy-start(f32[1,1,512]{2,1,0:T(1,128)} %get-tuple-element.149) | copy-start | bytes 6148
  117.5 5.0 %copy-start.7 = (f32[1,1,512]{2,1,0:T(1,128)S(1)}, f32[1,1,512]{2,1,0:T(1,128)}, u32[]{:S(2)}) copy-start(f32[1,1,512]{2,1,0:T(1,128)} %get-tuple-element.153) | copy-start | bytes 6148
  117.5 5.0 %copy-start.9 = (f32[1,1,512]{2,1,0:T(1,128)S(1)}, f32[1,1,512]{2,1,0:T(1,128)}, u32[]{:S(2)}) copy-start(f32[1,1,512]{2,1,0:T(1,128)} %get-tuple-element.148) | copy-start | bytes 6148
  117.5 5.0 %copy-start.11 = (f32[1,1,512]{2,1,0:T(1,128)S(1)}, f32[1,1,512]{2,1,0:T(1,128)}, u32[]{:S(2)}) copy-start(f32[1,1,512]{2,1,0:T(1,128)} %get-tuple-element.147) | copy-start | bytes 6148
  117.5 5.0 %copy-start.12 = (f32[1,1,512]{2,1,0:T(1,128)S(1)}, f32[1,1,512]{2,1,0:T(1,128)}, u32[]{:S(2)}) copy-start(f32[1,1,512]{2,1,0:T(1,128)} %get-tuple-element.152) | copy-start | bytes 6148
  117.5 5.0 %copy-start.14 = (f32[1,1,512]{2,1,0:T(1,128)S(1)}, f32[1,1,512]{2,1,0:T(1,128)}, u32[]{:S(2)}) copy-start(f32[1,1,512]{2,1,0:T(1,128)} %get-tuple-element.146) | copy-start | bytes 6148
  117.5 5.0 %copy-start.16 = (f32[1,1,512]{2,1,0:T(1,128)S(1)}, f32[1,1,512]{2,1,0:T(1,128)}, u32[]{:S(2)}) copy-start(f32[1,1,512]{2,1,0:T(1,128)} %get-tuple-element.145) | copy-start | bytes 6148
  117.5 5.0 %copy-start.18 = (f32[1,1,512]{2,1,0:T(1,128)S(1)}, f32[1,1,512]{2,1,0:T(1,128)}, u32[]{:S(2)}) copy-start(f32[1,1,512]{2,1,0:T(1,128)} %get-tuple-element.144) | copy-start | bytes 6148
  117.6 5.0 %copy-start.20 = (f32[1,1,512]{2,1,0:T(1,128)S(1)}, f32[1,1,512]{2,1,0:T(1,128)}, u32[]{:S(2)}) copy-start(f32[1,1,512]{2,1,0:T(1,128)} %get-tuple-element.143) | copy-start | bytes 6148
  117.6 5.0 %copy-start.22 = (f32[1,1,512]{2,1,0:T(1,128)S(1)}, f32[1,1,512]{2,1,0:T(1,128)}, u32[]{:S(2)}) copy-start(f32[1,1,512]{2,1,0:T(1,128)} %get-tuple-element.142) | copy-start | bytes 6148
  117.6 5.0 %copy-start.23 = (f32[1,1,512]{2,1,0:T(1,128)S(1)}, f32[1,1,512]{2,1,0:T(1,128)}, u32[]{:S(2)}) copy-start(f32[1,1,512]{2,1,0:T(1,128)} %get-tuple-element.151) | copy-start | bytes 6148
  121.0 1.8 copy-start.27
  121.0 1.8 copy-start.29
  121.0 2.2 copy-start.30
  121.0 2.2 copy-start.31
  121.0 2.2 copy-start.32
  121.0 2.2 copy-start.33
  121.0 2.2 copy-start.34
  121.1 2.2 copy-start.35
  121.1 2.2 copy-start.36
  121.1 2.2 copy-start.37
  121.1 2.2 copy-start.38
  123.3 1.1 copy-start.28
  126.4 2.5 copy-start.25
  181.6 5.9 %copy-start.3 = (f32[9,9,128]{2,1,0:T(8,128)S(1)}, f32[9,9,128]{2,1,0:T(8,128)}, u32[]{:S(2)}) copy-start(f32[9,9,128]{2,1,0:T(8,128)} %param.10) | copy-start | bytes 124420
  183.0 21.0 %all-to-all-start.4 = ((bf16[16,2,9,1024]{3,1,2,0:T(2,128)(2,1)}), bf16[16,2,9,1024]{3,1,2,0:T(2,128)(2,1)S(1)}, u32[]{:S(2)}, u32[]{:S(2)}) async-start(bf16[16,2,9,1024]{3,1,2,0:T(2,128)(2,1)} %copy.312), calls=%async_computation.4 | async-start | bytes 1179648 | tf_op jit(solution)/shard_map/all_to_all | solution.py:130
  315.3 48.8 %copy-start = (f32[32,9,128]{2,0,1:T(8,128)}, f32[32,9,128]{2,0,1:T(8,128)S(1)}, u32[]{:S(2)}) copy-start(f32[32,9,128]{2,0,1:T(8,128)S(1)} %copy.323) | copy-start | bytes 442372
where the time goes:
time: 367 us; the launch traced here: 364 us
  local copies, waits for them, and re-layouts  162 us (44%)
  other arithmetic  98.6 us (27%)
  blocking collectives  51.6 us (14%)
  waiting for transfers between devices  29.4 us (8%)
  starting transfers between devices  16.3 us (4%)
  matrix products  3.84 us (1%)
    scatter-add x1, other arithmetic, on_device(): incoming = jnp.zeros((columns, params, table_width + 1), jnp.float32).at[...  81.1 us
    scatter x1, local copies, waits for them, and re-layouts, on_device(): buffer = jnp.zeros((params, columns, buffer_slots), jnp.bfloat16).at[:, :...  47.4 us
    psum x1, blocking collectives, on_device(): lax.psum(gram_local, ('track', 'cam')) / row_total  39.5 us
    gather x10, local copies, waits for them, and re-layouts, on_device(): first_index = jnp.searchsorted(ranked, ranked, side='left')  34.9 us
    convert_element_type x4, local copies, waits for them, and re-layouts, on_device(): terms = arrived.reshape(track_count, cam_count, params, capacity, columns...  23.6 us
    all_to_all x1, waiting for transfers between devices, on_device(): lax.all_to_all(packed, 'track', split_axis=0, concat_axis=0, tiled=True)  15 us
    all_to_all x1, starting transfers between devices, on_device(): lax.all_to_all(request, 'track', split_axis=0, concat_axis=0, tiled=True)  8.34 us
    gather x1, local copies, waits for them, and re-layouts, on_device(): gathered_rows = jnp.take(omega, local_ids, axis=2)  8.28 us
  transfers between devices with their start and end apart: 3, of which 3 were waited for; matrix products, arithmetic and copies ran while one was open for 3% of the time, Pallas kernels for 0%

commit v1 on v0

v1 whole, which is shorter than its diff:
```python
import functools

import jax
import jax.numpy as jnp
from jax import lax
from jax.experimental import pallas as pl
from jax.experimental.pallas import tpu as pltpu
from jax.sharding import PartitionSpec as P

BLK_OBS = 128
TRK_BLK = 32
LANES = 128
CHUNK = 1024

HIGH = lax.Precision.HIGHEST
MESH = pl.DeviceIdType.MESH
NT = (((1,), (1,)), ((), ()))
F32 = jnp.float32
BF16 = jnp.bfloat16


def dot(left, right, precision=None):
    return jnp.dot(left, right, precision=precision, preferred_element_type=F32)


def dot_nt(left, right, precision=None):
    return lax.dot_general(left, right, NT, precision=precision, preferred_element_type=F32)


def one_hot(condition):
    return jnp.where(condition, 1.0, 0.0).astype(BF16)


def rows_iota(shape):
    return lax.broadcasted_iota(jnp.int32, shape, 0)


def lanes_iota(shape):
    return lax.broadcasted_iota(jnp.int32, shape, 1)


def repeat(count, body):
    if count == 1:
        body(0)
    else:
        pl.loop(0, count)(body)


def kernel(
    sizes,
    omega_ref, u_ref, rows_ref, ints_ref, v_ref,
    sketch_ref, basis_ref, factor_ref,
    send1, recv1, send2, recv2, send3, recv3, gsend, grecv,
    to_track, from_track, wide, pick, own, incoming, sum_ref,
    send_sems, recv_sems,
):
    track_count, cam_count, params, columns, capacity, chunk = sizes
    devices = track_count * cam_count
    cam_width = omega_ref.shape[1]
    obs_count = rows_ref.shape[1]
    tracks = v_ref.shape[2]
    chunks = devices * capacity // chunk
    per_chunk = chunk // capacity
    me = lax.axis_index("track") * cam_count + lax.axis_index("cam")

    def peer(step):
        other = lax.rem(me + step, devices)
        return other, (other // cam_count, lax.rem(other, cam_count))

    barrier = pltpu.get_barrier_semaphore()

    @pl.loop(1, devices)
    def _(step):
        pl.semaphore_signal(barrier, inc=1, device_id=peer(step)[1], device_id_type=MESH)

    def scatter(index, src, dst):
        @pl.loop(1, devices)
        def _(step):
            other, where = peer(step)
            pltpu.make_async_remote_copy(
                src_ref=src.at[other],
                dst_ref=dst.at[me],
                send_sem=send_sems.at[index],
                recv_sem=recv_sems.at[index],
                device_id=where,
                device_id_type=MESH,
            ).start()

        pltpu.make_async_copy(src.at[me], dst.at[me], recv_sems.at[index]).start()

    def broadcast(index, src, dst):
        @pl.loop(1, devices)
        def _(step):
            pltpu.make_async_remote_copy(
                src_ref=src,
                dst_ref=dst.at[me],
                send_sem=send_sems.at[index],
                recv_sem=recv_sems.at[index],
                device_id=peer(step)[1],
                device_id_type=MESH,
            ).start()

        pltpu.make_async_copy(src, dst.at[me], recv_sems.at[index]).start()

    def arrive(index, dst):
        pltpu.make_async_copy(dst, dst, recv_sems.at[index]).wait()

    def sent(index, dst):
        part = dst.at[pl.ds(0, devices - 1)]
        pltpu.make_async_copy(part, part, send_sems.at[index]).wait()

    owner = ints_ref[0:1, :]
    track_id = ints_ref[1:2, :]
    owned = one_hot(rows_iota((devices, obs_count)) == owner)
    earlier = one_hot(rows_iota((obs_count, obs_count)) < lanes_iota((obs_count, obs_count)))
    ranks = dot(owned, earlier)
    rank = jnp.sum(ranks * owned.astype(F32), axis=0, keepdims=True).astype(jnp.int32)
    slot = owner * capacity + rank
    member = one_hot(rows_iota((tracks, obs_count)) == track_id)
    fields = rows_ref[...]
    fields = jnp.concatenate(
        [fields, jnp.zeros((LANES - fields.shape[0], obs_count), BF16)], axis=0
    )

    def place(part):
        slots = one_hot(rows_iota((chunk, obs_count)) + part * chunk == slot)
        send1[pl.ds(part * per_chunk, per_chunk)] = (
            dot_nt(slots, fields).astype(BF16).reshape(per_chunk, capacity, LANES)
        )
        to_track[part] = dot_nt(member, slots).astype(BF16)
        from_track[part] = dot_nt(slots, member).astype(BF16)

    repeat(chunks, place)

    pl.semaphore_wait(barrier, devices - 1)
    scatter(0, send1, recv1)

    for row in range(params):
        total = jnp.zeros((columns, cam_width), F32)
        for col in range(params):
            total += u_ref[row, col : col + 1, :] * omega_ref[
                col * columns : (col + 1) * columns, :
            ].astype(F32)
        own[row * columns : (row + 1) * columns, :] = total
    incoming[...] = jnp.zeros_like(incoming)

    eye = one_hot(rows_iota((LANES, LANES)) == lanes_iota((LANES, LANES)))
    field_count = rows_ref.shape[0]
    width = 3 * columns

    def project(part):
        block = recv1[pl.ds(part * per_chunk, per_chunk)].reshape(chunk, LANES)
        turned = dot_nt(eye[:field_count], block)
        wide[part] = turned
        number = turned[3 * params : 3 * params + 1] * 256.0 + turned[
            3 * params + 1 : 3 * params + 2
        ]
        chosen = one_hot(rows_iota((cam_width, chunk)) == number.astype(jnp.int32))
        pick[part] = chosen
        gathered = dot(omega_ref[...], chosen)
        pieces = []
        for comp in range(3):
            total = jnp.zeros((columns, chunk), F32)
            for row in range(params):
                at = comp * params + row
                total += turned[at : at + 1] * gathered[row * columns : (row + 1) * columns]
            pieces.append(total)
        if width < LANES:
            pieces.append(jnp.zeros((LANES - width, chunk), F32))
        projected = jnp.concatenate(pieces, axis=0)
        send2[pl.ds(part * per_chunk, per_chunk)] = (
            projected.T.astype(BF16).reshape(per_chunk, capacity, LANES)
        )

    arrive(0, recv1)
    repeat(chunks, project)
    scatter(1, send2, recv2)
    sum_ref[...] = jnp.zeros_like(sum_ref)

    def collect(part):
        block = recv2[pl.ds(part * per_chunk, per_chunk)].reshape(chunk, LANES)
        sum_ref[...] += dot(to_track[part], block)

    arrive(1, recv2)
    repeat(chunks, collect)
    summed = sum_ref[...].T
    pieces = []
    for row in range(3):
        total = jnp.zeros((columns, tracks), F32)
        for col in range(3):
            total += v_ref[row, col : col + 1, :] * summed[col * columns : (col + 1) * columns]
        pieces.append(total)
    if width < LANES:
        pieces.append(jnp.zeros((LANES - width, tracks), F32))
    solved = jnp.concatenate(pieces, axis=0).astype(BF16)

    def spread(part):
        send3[pl.ds(part * per_chunk, per_chunk)] = (
            dot_nt(from_track[part], solved).astype(BF16).reshape(per_chunk, capacity, LANES)
        )

    repeat(chunks, spread)
    scatter(2, send3, recv3)

    def gather_back(part):
        block = recv3[pl.ds(part * per_chunk, per_chunk)].reshape(chunk, LANES)
        turned = dot_nt(eye[:width], block)
        weights = wide[part]
        pieces = []
        for row in range(params):
            total = jnp.zeros((columns, chunk), F32)
            for comp in range(3):
                at = comp * params + row
                total += weights[at : at + 1] * turned[comp * columns : (comp + 1) * columns]
            pieces.append(total)
        contribution = jnp.concatenate(pieces, axis=0).astype(BF16)
        incoming[...] += dot_nt(contribution, pick[part])

    arrive(2, recv3)
    repeat(chunks, gather_back)

    sketch = own[...] - incoming[...]
    sketch_ref[...] = sketch
    flat = jnp.concatenate(
        [sketch[row * columns : (row + 1) * columns] for row in range(params)], axis=1
    )
    gram = dot_nt(flat, flat, HIGH)
    groups = LANES // columns
    tall = columns // groups
    gsend[...] = jnp.concatenate(
        [gram[part * tall : (part + 1) * tall] for part in range(groups)], axis=1
    )
    broadcast(3, gsend, grecv)
    arrive(3, grecv)
    packed = jnp.sum(grecv[...], axis=0)
    gram = jnp.concatenate(
        [packed[:, part * columns : (part + 1) * columns] for part in range(groups)], axis=0
    )
    work = jnp.concatenate(
        [
            gram / (params * cam_width * devices),
            jnp.where(
                rows_iota((columns, columns)) == lanes_iota((columns, columns)), 1.0, 0.0
            ),
        ],
        axis=1,
    )
    row_ids = rows_iota((columns, 1))
    for step in range(columns - 1):
        scale = work[:, step : step + 1] * (1.0 / work[step : step + 1, step : step + 1])
        work = work - jnp.where(row_ids > step, scale, 0.0) * work[step : step + 1]
    upper = work[:, :columns]
    on_diagonal = rows_iota((columns, columns)) == lanes_iota((columns, columns))
    on_upper = rows_iota((columns, columns)) <= lanes_iota((columns, columns))
    diagonal = jnp.sum(jnp.where(on_diagonal, upper, 0.0), axis=1, keepdims=True)
    root = 1.0 / jnp.sqrt(diagonal)
    factor_ref[...] = jnp.where(on_upper, upper * root, 0.0)
    inverse = work[:, columns:] * root
    basis = dot(inverse, flat, HIGH)
    for row in range(params):
        basis_ref[row * columns : (row + 1) * columns, :] = basis[
            :, row * cam_width : (row + 1) * cam_width
        ]

    sent(0, recv1)
    sent(1, recv2)
    sent(2, recv3)
    sent(3, grecv)


def on_device(omega, u_blocks, w_blocks, v_inverse, obs_camera, obs_track, obs_mask):
    track_count = lax.axis_size("track")
    cam_count = lax.axis_size("cam")
    devices = track_count * cam_count
    columns, params, cam_width = omega.shape
    obs_count = obs_camera.shape[0]
    tracks = v_inverse.shape[2]
    capacity = max(2, 2 * obs_count // devices)
    capacity = -(-capacity // 16) * 16
    slots = devices * capacity
    chunk = min(CHUNK, slots)
    chunks = slots // chunk

    table = omega.transpose(1, 0, 2).reshape(params * columns, cam_width)
    owner = obs_camera // cam_width
    local = obs_camera - owner * cam_width
    weights = w_blocks.transpose(1, 0, 2).reshape(3 * params, obs_count)
    weights = weights * obs_mask.astype(BF16)
    number = jnp.stack([local // 256, local % 256]).astype(BF16)
    fields = jnp.concatenate([weights, number], axis=0)
    fields = jnp.pad(fields, ((0, 32 - fields.shape[0]), (0, 0)))
    block = jnp.arange(obs_count, dtype=jnp.int32) // BLK_OBS
    ints = jnp.stack([owner, block * TRK_BLK + obs_track])

    sizes = (track_count, cam_count, params, columns, capacity, chunk)
    message = pltpu.VMEM((devices, capacity, LANES), BF16)
    tall = columns * columns // LANES
    sketch, basis, factor = pl.pallas_call(
        functools.partial(kernel, sizes),
        out_shape=(
            jax.ShapeDtypeStruct((params * columns, cam_width), F32),
            jax.ShapeDtypeStruct((params * columns, cam_width), F32),
            jax.ShapeDtypeStruct((columns, columns), F32),
        ),
        in_specs=[pl.BlockSpec(memory_space=pltpu.VMEM)] * 5,
        out_specs=(pl.BlockSpec(memory_space=pltpu.VMEM),) * 3,
        scratch_shapes=[message] * 6
        + [
            pltpu.VMEM((tall, LANES), F32),
            pltpu.VMEM((devices, tall, LANES), F32),
            pltpu.VMEM((chunks, tracks, chunk), BF16),
            pltpu.VMEM((chunks, chunk, tracks), BF16),
            pltpu.VMEM((chunks, 32, chunk), F32),
            pltpu.VMEM((chunks, cam_width, chunk), BF16),
            pltpu.VMEM((params * columns, cam_width), F32),
            pltpu.VMEM((params * columns, cam_width), F32),
            pltpu.VMEM((tracks, LANES), F32),
            pltpu.SemaphoreType.DMA((4,)),
            pltpu.SemaphoreType.DMA((4,)),
        ],
        compiler_params=pltpu.CompilerParams(collective_id=0, has_side_effects=True),
    )(table, u_blocks, fields, ints, v_inverse)

    def unfold(array):
        return array.reshape(params, columns, cam_width).transpose(1, 0, 2)

    return (unfold(sketch), unfold(basis), factor)


def solution(mesh):
    spread = P(None, None, ("track", "cam"))
    flat = P(("track", "cam"))
    return jax.shard_map(
        on_device,
        mesh=mesh,
        in_specs=(spread,) * 4 + (flat,) * 3,
        out_specs=(spread, spread, P()),
        check_vma=False,
    )
```

time: 367 us -> 49.8 us (0.14)
  local copies, waits for them, and re-layouts: 162 us -> 3.65 us
  other arithmetic: 98.6 us -> 3.32 us
  blocking collectives: 51.6 us -> 0 us
  Pallas kernels: 0 us -> 41.8 us
  waiting for transfers between devices: 29.4 us -> 0 us
  starting transfers between devices: 16.3 us -> 0 us
  matrix products: 3.84 us -> 0 us
    scatter-add x1 -> x0, other arithmetic: 81.1 us -> none  [on_device(): incoming = jnp.zeros((columns, params, table_width + 1), jnp.float32).at[...]
    scatter x3 -> x0, local copies, waits for them, and re-layouts: 52.4 us -> none  [the longest x1 47.4 us: on_device(): buffer = jnp.zeros((params, columns, buffer_slots), jnp.bfloat16).at[:, :...]
    gather x14 -> x0, local copies, waits for them, and re-layouts: 51.3 us -> none  [the longest x10 34.9 us: on_device(): first_index = jnp.searchsorted(ranked, ranked, side='left')]
    pallas_call x0 -> x1, Pallas kernels: none -> 41.8 us  [on_device(): pl.pallas_call(functools.partial(kernel, sizes), out_shape=(jax.ShapeDtyp...]
    psum x1 -> x0, blocking collectives: 39.5 us -> none  [on_device(): lax.psum(gram_local, ('track', 'cam')) / row_total]
    all_to_all x3 -> x0, waiting for transfers between devices: 29.4 us -> none  [the longest x1 15 us: on_device(): lax.all_to_all(packed, 'track', split_axis=0, concat_axis=0, tiled=True)]
    convert_element_type x5 -> x0, local copies, waits for them, and re-layouts: 25.5 us -> none  [the longest x4 23.6 us: on_device(): terms = arrived.reshape(track_count, cam_count, params, capacity, columns...]
    reshape x10 -> x1, local copies, waits for them, and re-layouts: 18.2 us -> 0.02 us  [on_device(): weights = w_blocks.transpose(1, 0, 2).reshape(3 * params, obs_count)]
  transfers between devices with their start and end apart: 3 -> 0, of which waited for: 3 -> 0; matrix products, arithmetic and copies ran while one was open for 3% -> 0% of each run, Pallas kernels for 0% -> 0%
where the time goes in v1:
time: 49.8 us; the launch traced here: 49.5 us
  Pallas kernels  41.8 us (84%)
  local copies, waits for them, and re-layouts  3.65 us (7%)
  other arithmetic  3.32 us (7%)
  between operations  0.69 us (1%)
    pallas_call x1, Pallas kernels, on_device(): pl.pallas_call(functools.partial(kernel, sizes), out_shape=(jax.ShapeDtyp...  41.8 us
    unnamed x11, local copies, waits for them, and re-layouts  3.61 us
    another operation x2, other arithmetic  1.4 us

profile of v1, /device:TPU:0, one launch (start us, length us, event | category | flops | bytes accessed | tf_op | source)
XLA Modules:
  0.0 49.5 jit_solution(17928399986836226482)
XLA Ops:
  0.6 0.0 copy-start.3
  0.6 0.0 copy-start.1
  0.7 0.7 %copy-done.3 = s32[512]{0:T(512)S(1)} copy-done((s32[512]{0:T(512)S(1)}, s32[512]{0:T(512)}, u32[]{:S(2)}) %copy-start.3) | copy-done | bytes 2072
  1.3 0.7 %fusion.9 = s32[512]{0:T(512)S(1)} fusion(s32[512]{0:T(512)} %param.12), kind=kLoop, calls=%fused_computation.25 | loop fusion | flops 5120 | bytes 4096 | tf_op jit(solution)/shard_map/add | solution.py:293
  2.0 0.7 %fusion.6 = (bf16[512]{0:T(512)(128)(2,1)S(1)}, s32[512]{0:T(512)S(1)}) fusion(s32[512]{0:T(512)} %param.11), kind=kLoop, calls=%fused_computation.22 | loop fusion | flops 16896 | bytes 5120 | tf_op jit(solution)/shard_map/convert.3
  2.7 0.7 %fusion.7 = bf16[512]{0:T(512)(128)(2,1)S(1)} fusion(s32[512]{0:T(512)} %param.11, s32[512]{0:T(512)S(1)} %get-tuple-element.10), kind=kLoop, calls=%fused_computation.23 | loop fusion | flops 7168 | bytes 5120 | tf_op jit(solution)/shard_map/convert.2
  3.4 0.6 %pad_add_fusion.ints_ref = s32[2,512]{1,0:T(2,128)} fusion(s32[1,512]{1,0:T(1,128)S(1)} %bitcast.17, s32[1,512]{1,0:T(1,128)S(1)} %bitcast.16), kind=kLoop, calls=%fused_computation.7 | loop fusion | flops 1024 | bytes 8192 | tf_op jit(solution)/shard_map/stack | solution.py:293
  4.0 0.0 copy-done.1
  4.1 0.6 %fusion.4.rows_ref = bf16[32,512]{1,0:T(8,128)(2,1)} fusion(bf16[1,512]{1,0:T(2,128)(2,1)S(1)} %stack.20, bf16[1,512]{1,0:T(2,128)(2,1)S(1)} %stack.19, bf16[27,512]{1,0:T(8,128)(2,1)S(1)} %broadcast_multiply_fusion), kind=kLoop, calls=%fused_computation.5 | loop fusion | flops 163840 | bytes 62464 | tf_op jit(solution)/shard_map/concatenate | solution.py:290
  4.7 41.8 %shard_map.94 = (f32[288,128]{1,0:T(8,128)}, f32[288,128]{1,0:T(8,128)}, f32[32,32]{1,0:T(8,128)}) custom-call(bf16[288,128]{1,0:T(8,128)(2,1)} %bitcast.14, f32[9,9,128]{2,1,0:T(8,128)} %u_ref.1, bf16[32,512]{1,0:T(8,128)(2,1)} %fusion.4.rows_ref, s32[2,512]{1,0:T(2,128)} %pad_add_fusion.ints_ref, f32[3,3,128]{2,1,0:T(4,128)} %v_ref.1), custom_call_target="tpu_custom_call" | custom-call | tf_op jit(solution)/shard_map/pallas_call | solution.py:298
  46.5 0.0 copy-start
  46.5 1.6 %copy.15 = f32[32,9,128]{2,0,1:T(8,128)} copy(f32[32,9,128]{2,0,1:T(8,128)} %bitcast.13) | data formatting | bytes 294912
  48.2 0.0 copy-done
  48.2 0.0 copy-start.2
  48.2 0.7 %copy.16 = f32[32,9,128]{2,0,1:T(8,128)} copy(f32[32,9,128]{2,0,1:T(8,128)S(1)} %bitcast.12) | data formatting | bytes 294912
  48.8 0.1 copy-done.2
  48.9 0.6 %copy.17 = f32[32,32]{1,0:T(8,128)} copy(f32[32,32]{1,0:T(8,128)S(1)} %copy-done.2) | data formatting | bytes 8192
  (6 shorter events, 0.1 us)
Async XLA Ops:
  0.6 0.7 %copy-start.3 = (s32[512]{0:T(512)S(1)}, s32[512]{0:T(512)}, u32[]{:S(2)}) copy-start(s32[512]{0:T(512)} %param.13) | copy-start | bytes 6148
  0.6 3.4 %copy-start.1 = (bf16[9,3,512]{2,1,0:T(4,128)(2,1)S(1)}, bf16[9,3,512]{2,1,0:T(4,128)(2,1)}, u32[]{:S(2)}) copy-start(bf16[9,3,512]{2,1,0:T(4,128)(2,1)} %param.9) | copy-start | bytes 82948
  46.5 1.6 %copy-start = (f32[288,128]{1,0:T(8,128)S(1)}, f32[288,128]{1,0:T(8,128)}, u32[]{:S(2)}) copy-start(f32[288,128]{1,0:T(8,128)} %get-tuple-element.7) | copy-start | bytes 442372
  48.2 0.7 %copy-start.2 = (f32[32,32]{1,0:T(8,128)S(1)}, f32[32,32]{1,0:T(8,128)}, u32[]{:S(2)}) copy-start(f32[32,32]{1,0:T(8,128)} %get-tuple-element.16) | copy-start | bytes 12292

commit v2 on v1

v2 whole, which is shorter than its diff:
```python
import functools

import jax
import jax.numpy as jnp
from jax import lax
from jax.experimental import pallas as pl
from jax.experimental.pallas import tpu as pltpu
from jax.sharding import PartitionSpec as P

BLK_OBS = 128
TRK_BLK = 32
LANES = 128
CHUNK = 1024

HIGH = lax.Precision.HIGHEST
MESH = pl.DeviceIdType.MESH
NT = (((1,), (1,)), ((), ()))
F32 = jnp.float32
BF16 = jnp.bfloat16


def dot(left, right, precision=None):
    return jnp.dot(left, right, precision=precision, preferred_element_type=F32)


def dot_nt(left, right, precision=None):
    return lax.dot_general(left, right, NT, precision=precision, preferred_element_type=F32)


def one_hot(condition):
    return jnp.where(condition, 1.0, 0.0).astype(BF16)


def rows_iota(shape):
    return lax.broadcasted_iota(jnp.int32, shape, 0)


def lanes_iota(shape):
    return lax.broadcasted_iota(jnp.int32, shape, 1)


def repeat(count, body):
    if count == 1:
        body(0)
    else:
        pl.loop(0, count)(body)


def kernel(
    sizes,
    omega_ref, u_ref, w_ref, v_ref, camera_ref, track_ref, mask_ref,
    sketch_ref, basis_ref, factor_ref,
    send1, recv1, send2, recv2, send3, recv3, gsend, grecv,
    fields, to_track, wide, pick, own, incoming, sum_ref,
    send_sems, recv_sems,
):
    track_count, cam_count, params, columns, rows, groups, span = sizes
    devices = track_count * cam_count
    cam_width = omega_ref.shape[1]
    obs_count = camera_ref.shape[1]
    tracks = v_ref.shape[2]
    part_rows = span * rows
    chunk = groups * part_rows
    chunks = devices // span
    me = lax.axis_index("track") * cam_count + lax.axis_index("cam")

    def peer(turn):
        step = devices // 2 + (1 - 2 * lax.rem(turn, 2)) * ((turn + 1) // 2)
        other = lax.rem(me + step, devices)
        return other, (other // cam_count, lax.rem(other, cam_count))

    barrier = pltpu.get_barrier_semaphore()

    @pl.loop(0, devices - 1)
    def _(turn):
        pl.semaphore_signal(barrier, inc=1, device_id=peer(turn)[1], device_id_type=MESH)

    def scatter(index, src, dst):
        @pl.loop(0, devices - 1)
        def _(turn):
            other, where = peer(turn)
            pltpu.make_async_remote_copy(
                src_ref=src.at[other],
                dst_ref=dst.at[me],
                send_sem=send_sems.at[index],
                recv_sem=recv_sems.at[index],
                device_id=where,
                device_id_type=MESH,
            ).start()

        pltpu.make_async_copy(src.at[me], dst.at[me], recv_sems.at[index]).start()

    def broadcast(index, src, dst):
        @pl.loop(0, devices - 1)
        def _(turn):
            pltpu.make_async_remote_copy(
                src_ref=src,
                dst_ref=dst.at[me],
                send_sem=send_sems.at[index],
                recv_sem=recv_sems.at[index],
                device_id=peer(turn)[1],
                device_id_type=MESH,
            ).start()

        pltpu.make_async_copy(src, dst.at[me], recv_sems.at[index]).start()

    def arrive(index, dst):
        pltpu.make_async_copy(dst, dst, recv_sems.at[index]).wait()

    def sent(index, dst):
        part = dst.at[pl.ds(0, devices - 1)]
        pltpu.make_async_copy(part, part, send_sems.at[index]).wait()

    eye = one_hot(rows_iota((LANES, LANES)) == lanes_iota((LANES, LANES)))

    def pack(part, values, dst):
        for index in range(values.shape[0] // columns):
            block = values[index * columns : (index + 1) * columns]
            pieces = [block[:, g * part_rows : (g + 1) * part_rows] for g in range(groups)]
            if groups * columns < LANES:
                pieces.append(jnp.zeros((LANES - groups * columns, part_rows), F32))
            turned = jnp.concatenate(pieces, axis=0).T.reshape(span, rows, LANES)
            dst[pl.ds(part * span, span), index * rows : (index + 1) * rows] = turned.astype(BF16)

    def unpack(part, src):
        blocks = []
        for index in range(src.shape[1] // rows):
            block = src[pl.ds(part * span, span), index * rows : (index + 1) * rows]
            turned = dot_nt(eye, block.reshape(part_rows, LANES))
            blocks.append(
                jnp.concatenate(
                    [turned[g * columns : (g + 1) * columns] for g in range(groups)], axis=1
                )
            )
        return jnp.concatenate(blocks, axis=0)

    camera = camera_ref[...]
    owner = camera // cam_width
    local = camera - owner * cam_width
    track_id = lanes_iota((1, obs_count)) // BLK_OBS * TRK_BLK + track_ref[...]
    live = mask_ref[...].astype(F32)
    fields[...] = jnp.zeros_like(fields)
    for row in range(params):
        fields[3 * row : 3 * row + 3, :] = w_ref[row].astype(F32) * live
    high = local // 256
    fields[3 * params : 3 * params + 1, :] = high.astype(F32)
    fields[3 * params + 1 : 3 * params + 2, :] = (local - high * 256).astype(F32)
    owned = one_hot(rows_iota((devices, obs_count)) == owner)
    earlier = one_hot(rows_iota((obs_count, obs_count)) < lanes_iota((obs_count, obs_count)))
    ranks = dot(owned, earlier)
    rank = jnp.sum(ranks * owned.astype(F32), axis=0, keepdims=True).astype(jnp.int32)
    group = jnp.zeros_like(rank)
    for g in range(1, groups):
        group += jnp.where(rank >= g * rows, 1, 0)
    offset = group * part_rows + rank - group * rows
    member = one_hot(rows_iota((tracks, obs_count)) == track_id)
    table = jnp.concatenate([fields[...].astype(BF16), member], axis=0)

    def place(part):
        nearby = owner - part * span
        inside = jnp.logical_and(nearby >= 0, nearby < span)
        slot = jnp.where(inside, nearby * rows + offset, -1)
        slots = one_hot(rows_iota((chunk, obs_count)) == slot)
        placed = dot_nt(table, slots)
        pack(part, placed[:columns], send1)
        to_track[part] = placed[columns:].astype(BF16)

    repeat(chunks, place)

    pl.semaphore_wait(barrier, devices - 1)
    scatter(0, send1, recv1)

    for row in range(params):
        total = jnp.zeros((columns, cam_width), F32)
        for col in range(params):
            total += u_ref[row, col : col + 1, :] * omega_ref[
                col * columns : (col + 1) * columns, :
            ].astype(F32)
        own[row * columns : (row + 1) * columns, :] = total
    incoming[...] = jnp.zeros_like(incoming)
    sum_ref[...] = jnp.zeros_like(sum_ref)

    def project(part):
        turned = unpack(part, recv1)
        wide[part] = turned
        number = turned[3 * params : 3 * params + 1] * 256.0 + turned[
            3 * params + 1 : 3 * params + 2
        ]
        chosen = one_hot(rows_iota((cam_width, chunk)) == number.astype(jnp.int32))
        pick[part] = chosen
        gathered = dot(omega_ref[...], chosen)
        pieces = []
        for comp in range(3):
            total = jnp.zeros((columns, chunk), F32)
            for row in range(params):
                at = row * 3 + comp
                total += turned[at : at + 1] * gathered[row * columns : (row + 1) * columns]
            pieces.append(total)
        pack(part, jnp.concatenate(pieces, axis=0), send2)

    arrive(0, recv1)
    repeat(chunks, project)
    scatter(1, send2, recv2)

    def collect(part):
        sum_ref[...] += dot_nt(unpack(part, recv2).astype(BF16), to_track[part])

    arrive(1, recv2)
    repeat(chunks, collect)
    pieces = []
    for row in range(3):
        total = jnp.zeros((columns, tracks), F32)
        for col in range(3):
            total += v_ref[row, col : col + 1, :] * sum_ref[col * columns : (col + 1) * columns]
        pieces.append(total)
    solved = jnp.concatenate(pieces, axis=0).astype(BF16)

    def spread(part):
        pack(part, dot(solved, to_track[part]), send3)

    repeat(chunks, spread)
    scatter(2, send3, recv3)

    def gather_back(part):
        turned = unpack(part, recv3)
        weights = wide[part]
        pieces = []
        for row in range(params):
            total = jnp.zeros((columns, chunk), F32)
            for comp in range(3):
                at = row * 3 + comp
                total += weights[at : at + 1] * turned[comp * columns : (comp + 1) * columns]
            pieces.append(total)
        contribution = jnp.concatenate(pieces, axis=0).astype(BF16)
        incoming[...] += dot_nt(contribution, pick[part])

    arrive(2, recv3)
    repeat(chunks, gather_back)

    sketch = own[...] - incoming[...]
    sketch_ref[...] = sketch
    flat = jnp.concatenate(
        [sketch[row * columns : (row + 1) * columns] for row in range(params)], axis=1
    )
    gram = dot_nt(flat, flat, HIGH)
    folds = LANES // columns
    tall = columns // folds
    gsend[...] = jnp.concatenate(
        [gram[part * tall : (part + 1) * tall] for part in range(folds)], axis=1
    )
    broadcast(3, gsend, grecv)
    arrive(3, grecv)
    packed = jnp.sum(grecv[...], axis=0)
    gram = jnp.concatenate(
        [packed[:, part * columns : (part + 1) * columns] for part in range(folds)], axis=0
    )
    work = jnp.concatenate(
        [
            gram / (params * cam_width * devices),
            jnp.where(
                rows_iota((columns, columns)) == lanes_iota((columns, columns)), 1.0, 0.0
            ),
        ],
        axis=1,
    )
    row_ids = rows_iota((columns, 1))
    for step in range(columns - 1):
        scale = work[:, step : step + 1] * (1.0 / work[step : step + 1, step : step + 1])
        work = work - jnp.where(row_ids > step, scale, 0.0) * work[step : step + 1]
    upper = work[:, :columns]
    on_diagonal = rows_iota((columns, columns)) == lanes_iota((columns, columns))
    on_upper = rows_iota((columns, columns)) <= lanes_iota((columns, columns))
    diagonal = jnp.sum(jnp.where(on_diagonal, upper, 0.0), axis=1, keepdims=True)
    root = 1.0 / jnp.sqrt(diagonal)
    factor_ref[...] = jnp.where(on_upper, upper * root, 0.0)
    inverse = work[:, columns:] * root
    basis = dot(inverse, flat, HIGH)
    for row in range(params):
        basis_ref[row * columns : (row + 1) * columns, :] = basis[
            :, row * cam_width : (row + 1) * cam_width
        ]

    sent(0, recv1)
    sent(1, recv2)
    sent(2, recv3)
    sent(3, grecv)


def on_device(omega, u_blocks, w_blocks, v_inverse, obs_camera, obs_track, obs_mask):
    track_count = lax.axis_size("track")
    cam_count = lax.axis_size("cam")
    devices = track_count * cam_count
    columns, params, cam_width = omega.shape
    obs_count = obs_camera.shape[0]
    tracks = v_inverse.shape[2]
    capacity = max(2, 2 * obs_count // devices)
    rows = -(-capacity // (LANES // columns) // 8) * 8
    groups = -(-capacity // rows)
    span = devices
    while span * rows * groups > CHUNK and span % 2 == 0:
        span //= 2
    chunk = span * rows * groups
    chunks = devices // span

    table = omega.transpose(1, 0, 2).reshape(params * columns, cam_width)
    line = (1, obs_count)
    sizes = (track_count, cam_count, params, columns, rows, groups, span)
    small = pltpu.VMEM((devices, rows, LANES), BF16)
    message = pltpu.VMEM((devices, 3 * rows, LANES), BF16)
    tall = columns * columns // LANES
    sketch, basis, factor = pl.pallas_call(
        functools.partial(kernel, sizes),
        out_shape=(
            jax.ShapeDtypeStruct((params * columns, cam_width), F32),
            jax.ShapeDtypeStruct((params * columns, cam_width), F32),
            jax.ShapeDtypeStruct((columns, columns), F32),
        ),
        in_specs=[pl.BlockSpec(memory_space=pltpu.VMEM)] * 7,
        out_specs=(pl.BlockSpec(memory_space=pltpu.VMEM),) * 3,
        scratch_shapes=[small] * 2
        + [message] * 4
        + [
            pltpu.VMEM((tall, LANES), F32),
            pltpu.VMEM((devices, tall, LANES), F32),
            pltpu.VMEM((columns, obs_count), F32),
            pltpu.VMEM((chunks, tracks, chunk), BF16),
            pltpu.VMEM((chunks, columns, chunk), F32),
            pltpu.VMEM((chunks, cam_width, chunk), BF16),
            pltpu.VMEM((params * columns, cam_width), F32),
            pltpu.VMEM((params * columns, cam_width), F32),
            pltpu.VMEM((3 * columns, tracks), F32),
            pltpu.SemaphoreType.DMA((4,)),
            pltpu.SemaphoreType.DMA((4,)),
        ],
        compiler_params=pltpu.CompilerParams(collective_id=0, has_side_effects=True),
    )(
        table,
        u_blocks,
        w_blocks,
        v_inverse,
        obs_camera.reshape(line),
        obs_track.reshape(line),
        obs_mask.reshape(line),
    )

    def unfold(array):
        return array.reshape(params, columns, cam_width).transpose(1, 0, 2)

    return (unfold(sketch), unfold(basis), factor)


def solution(mesh):
    spread = P(None, None, ("track", "cam"))
    flat = P(("track", "cam"))
    return jax.shard_map(
        on_device,
        mesh=mesh,
        in_specs=(spread,) * 4 + (flat,) * 3,
        out_specs=(spread, spread, P()),
        check_vma=False,
    )
```

time: 49.8 us -> 42.4 us (0.85)
  other arithmetic: 3.32 us -> 0 us
  Pallas kernels: 41.8 us -> 38.6 us
  local copies, waits for them, and re-layouts: 3.65 us -> 2.94 us
    pallas_call x1, Pallas kernels: 41.8 us -> 38.6 us  [on_device(): pl.pallas_call(functools.partial(kernel, sizes), out_shape=(jax.ShapeDtyp...]
    another operation x3 -> x0, other arithmetic: 2 us -> none
    add x1 -> x0, other arithmetic: 0.69 us -> none  [on_device(): ints = jnp.stack([owner, block * TRK_BLK + obs_track])]
    unnamed x11 -> x7, local copies, waits for them, and re-layouts: 3.61 us -> 2.94 us
    concatenate x1 -> x0, other arithmetic: 0.63 us -> none  [on_device(): fields = jnp.concatenate([weights, number], axis=0)]
where the time goes in v2:
time: 42.4 us; the launch traced here: 42.2 us
  Pallas kernels  38.6 us (91%)
  local copies, waits for them, and re-layouts  2.94 us (7%)
  between operations  0.65 us (2%)
    pallas_call x1, Pallas kernels, on_device(): pl.pallas_call(functools.partial(kernel, sizes), out_shape=(jax.ShapeDtyp...  38.6 us
    unnamed x7, local copies, waits for them, and re-layouts  2.94 us

profile of v2, /device:TPU:0, one launch (start us, length us, event | category | flops | bytes accessed | tf_op | source)
XLA Modules:
  0.0 42.2 jit_solution(6519819924982773749)
XLA Ops:
  0.6 38.6 %shard_map.94 = (f32[288,128]{1,0:T(8,128)}, f32[288,128]{1,0:T(8,128)}, f32[32,32]{1,0:T(8,128)}) custom-call(bf16[288,128]{1,0:T(8,128)(2,1)} %bitcast.14, f32[9,9,128]{2,1,0:T(8,128)} %u_ref.1, bf16[9,3,512]{2,1,0:T(4,128)(2,1)} %w_ref.1, f32[3,3,128]{2,1,0:T(4,128)} %v_ref.1, s32[1,512]{1,0:T(1,128)} %bitcast.15, s32[1,512]{1,0:T(1,128)} %bitcast.16, ...), custom_call_target="tpu_custom_call" | custom-call | tf_op jit(solution)/shard_map/pallas_call | solution.py:311
  39.2 0.0 copy-start
  39.3 1.6 %copy.13 = f32[32,9,128]{2,0,1:T(8,128)} copy(f32[32,9,128]{2,0,1:T(8,128)} %bitcast.13) | data formatting | bytes 294912
  40.9 0.0 copy-done
  40.9 0.0 copy-start.1
  40.9 0.7 %copy.14 = f32[32,9,128]{2,0,1:T(8,128)} copy(f32[32,9,128]{2,0,1:T(8,128)S(1)} %bitcast.12) | data formatting | bytes 294912
  41.5 0.1 copy-done.1
  41.6 0.6 %copy.15 = f32[32,32]{1,0:T(8,128)} copy(f32[32,32]{1,0:T(8,128)S(1)} %copy-done.1) | data formatting | bytes 8192
Async XLA Ops:
  39.2 1.6 %copy-start = (f32[288,128]{1,0:T(8,128)S(1)}, f32[288,128]{1,0:T(8,128)}, u32[]{:S(2)}) copy-start(f32[288,128]{1,0:T(8,128)} %get-tuple-element.7) | copy-start | bytes 442372
  40.9 0.7 %copy-start.1 = (f32[32,32]{1,0:T(8,128)S(1)}, f32[32,32]{1,0:T(8,128)}, u32[]{:S(2)}) copy-start(f32[32,32]{1,0:T(8,128)} %get-tuple-element.14) | copy-start | bytes 12292

commit v3 on v2

--- a/solution.py
+++ b/solution.py
@@ -48,11 +48,12 @@
 
 def kernel(
     sizes,
-    omega_ref, u_ref, w_ref, v_ref, camera_ref, track_ref, mask_ref,
+    omega_hbm, u_hbm, w_hbm, v_hbm, camera_hbm, track_hbm, mask_hbm,
     sketch_ref, basis_ref, factor_ref,
     send1, recv1, send2, recv2, send3, recv3, gsend, grecv,
     fields, to_track, wide, pick, own, incoming, sum_ref,
     send_sems, recv_sems,
+    omega_ref, u_ref, w_ref, v_ref, camera_ref, track_ref, mask_ref, load_sems,
 ):
     track_count, cam_count, params, columns, rows, groups, span = sizes
     devices = track_count * cam_count
@@ -65,8 +66,7 @@
     me = lax.axis_index("track") * cam_count + lax.axis_index("cam")
 
     def peer(turn):
-        step = devices // 2 + (1 - 2 * lax.rem(turn, 2)) * ((turn + 1) // 2)
-        other = lax.rem(me + step, devices)
+        other = lax.rem(me + turn + 1, devices)
         return other, (other // cam_count, lax.rem(other, cam_count))
 
     barrier = pltpu.get_barrier_semaphore()
@@ -74,6 +74,23 @@
     @pl.loop(0, devices - 1)
     def _(turn):
         pl.semaphore_signal(barrier, inc=1, device_id=peer(turn)[1], device_id_type=MESH)
+
+    loads = [
+        pltpu.make_async_copy(source, target, load_sems.at[index])
+        for index, (source, target) in enumerate(
+            [
+                (camera_hbm, camera_ref),
+                (track_hbm, track_ref),
+                (mask_hbm, mask_ref),
+                (w_hbm, w_ref),
+                (omega_hbm, omega_ref),
+                (u_hbm, u_ref),
+                (v_hbm, v_ref),
+            ]
+        )
+    ]
+    for load in loads:
+        load.start()
 
     def scatter(index, src, dst):
         @pl.loop(0, devices - 1)
@@ -134,6 +151,8 @@
             )
         return jnp.concatenate(blocks, axis=0)
 
+    for load in loads[:4]:
+        load.wait()
     camera = camera_ref[...]
     owner = camera // cam_width
     local = camera - owner * cam_width
@@ -170,6 +189,8 @@
     pl.semaphore_wait(barrier, devices - 1)
     scatter(0, send1, recv1)
 
+    for load in loads[4:]:
+        load.wait()
     for row in range(params):
         total = jnp.zeros((columns, cam_width), F32)
         for col in range(params):
@@ -304,6 +325,15 @@
 
     table = omega.transpose(1, 0, 2).reshape(params * columns, cam_width)
     line = (1, obs_count)
+    operands = (
+        table,
+        u_blocks,
+        w_blocks,
+        v_inverse,
+        obs_camera.reshape(line),
+        obs_track.reshape(line),
+        obs_mask.reshape(line),
+    )
     sizes = (track_count, cam_count, params, columns, rows, groups, span)
     small = pltpu.VMEM((devices, rows, LANES), BF16)
     message = pltpu.VMEM((devices, 3 * rows, LANES), BF16)
@@ -311,11 +341,11 @@
     sketch, basis, factor = pl.pallas_call(
         functools.partial(kernel, sizes),
         out_shape=(
-            jax.ShapeDtypeStruct((params * columns, cam_width), F32),
-            jax.ShapeDtypeStruct((params * columns, cam_width), F32),
-            jax.ShapeDtypeStruct((columns, columns), F32),
+            pltpu.VMEM((params * columns, cam_width), F32),
+            pltpu.VMEM((params * columns, cam_width), F32),
+            pltpu.VMEM((columns, columns), F32),
         ),
-        in_specs=[pl.BlockSpec(memory_space=pltpu.VMEM)] * 7,
+        in_specs=[pl.BlockSpec(memory_space=pl.ANY)] * 7,
         out_specs=(pl.BlockSpec(memory_space=pltpu.VMEM),) * 3,
         scratch_shapes=[small] * 2
         + [message] * 4
@@ -331,17 +361,11 @@
             pltpu.VMEM((3 * columns, tracks), F32),
             pltpu.SemaphoreType.DMA((4,)),
             pltpu.SemaphoreType.DMA((4,)),
-        ],
+        ]
+        + [pltpu.VMEM(array.shape, array.dtype) for array in operands]
+        + [pltpu.SemaphoreType.DMA((len(operands),))],
         compiler_params=pltpu.CompilerParams(collective_id=0, has_side_effects=True),
-    )(
-        table,
-        u_blocks,
-        w_blocks,
-        v_inverse,
-        obs_camera.reshape(line),
-        obs_track.reshape(line),
-        obs_mask.reshape(line),
-    )
+    )(*operands)
 
     def unfold(array):
         return array.reshape(params, columns, cam_width).transpose(1, 0, 2)

time: 42.4 us -> 37.7 us (0.89)
  Pallas kernels: 38.6 us -> 35 us
  local copies, waits for them, and re-layouts: 2.94 us -> 1.93 us
    pallas_call x1, Pallas kernels: 38.6 us -> 35 us  [on_device(): pl.pallas_call(functools.partial(kernel, sizes), out_shape=(pltpu.VMEM((p...]
    unnamed x7 -> x3, local copies, waits for them, and re-layouts: 2.94 us -> 1.93 us
where the time goes in v3:
time: 37.7 us; the launch traced here: 37.6 us
  Pallas kernels  35 us (93%)
  local copies, waits for them, and re-layouts  1.93 us (5%)
  between operations  0.64 us (2%)
    pallas_call x1, Pallas kernels, on_device(): pl.pallas_call(functools.partial(kernel, sizes), out_shape=(pltpu.VMEM((p...  35 us
    unnamed x3, local copies, waits for them, and re-layouts  1.93 us

profile of v3, /device:TPU:0, one launch (start us, length us, event | category | flops | bytes accessed | tf_op | source)
XLA Modules:
  0.0 37.6 jit_solution(8437861023619010490)
XLA Ops:
  0.6 35.0 %shard_map.94 = (f32[288,128]{1,0:T(8,128)S(1)}, f32[288,128]{1,0:T(8,128)S(1)}, f32[32,32]{1,0:T(8,128)S(1)}) custom-call(bf16[288,128]{1,0:T(8,128)(2,1)} %bitcast.14, f32[9,9,128]{2,1,0:T(8,128)} %u_hbm.1, bf16[9,3,512]{2,1,0:T(4,128)(2,1)} %w_hbm.1, f32[3,3,128]{2,1,0:T(4,128)} %v_hbm.1, s32[1,512]{1,0:T(1,128)} %bitcast.15, s32[1,512]{1,0:T(1,128)} %bitcast.16, ...), custom_call_target="tpu_custom_call" | custom-call | tf_op jit(solution)/shard_map/pallas_call | solution.py:341
  35.6 0.7 %copy.13 = f32[32,9,128]{2,0,1:T(8,128)} copy(f32[32,9,128]{2,0,1:T(8,128)S(1)} %bitcast.13) | data formatting | bytes 294912
  36.3 0.7 %copy.14 = f32[32,9,128]{2,0,1:T(8,128)} copy(f32[32,9,128]{2,0,1:T(8,128)S(1)} %bitcast.12) | data formatting | bytes 294912
  36.9 0.6 %copy.15 = f32[32,32]{1,0:T(8,128)} copy(f32[32,32]{1,0:T(8,128)S(1)} %get-tuple-element.11) | data formatting | bytes 8192
